TPU v7x, 8 devices: a whole 2x2x1 slice. The times are simulated.
8 devices in a mesh: dp: 8 (over z, y, x, core).
Axes of the slice: x: 2, y: 2, z: 1, core: 2. Of those that a mesh axis runs over, the one named last changes fastest.
Arguments:
- img_emb: bfloat16 [16384, 1024], P('dp')
- txt_emb: bfloat16 [16384, 1024], P('dp')
- log_temp: float32 [], replicated
- logit_bias: float32 [], replicated
Outputs:
- output 1: float32 [], replicated
- output 2: float32 [16384, 1024], P('dp')
- output 3: float32 [16384, 1024], P('dp')
- output 4: float32 [], replicated
- output 5: float32 [], replicated
All inputs are finite; a program needn't handle non-finite values.
Results may differ from a plain program's by a relative error of at most 0.001.
Values are sent between devices in bfloat16 or wider.
A program may use at most 1 GiB of HBM per device.

v0:
```python
import jax
import jax.numpy as jnp
from jax import lax
from jax.sharding import PartitionSpec as P


def normalize_rows(emb):
    emb32 = emb.astype(jnp.float32)
    inv_norm = lax.rsqrt(jnp.sum(emb32 * emb32, axis=-1, keepdims=True))
    return emb32 * inv_norm, inv_norm


def project_back(unit_rows, inv_norm, grad_dir):
    radial = jnp.sum(unit_rows * grad_dir, axis=-1, keepdims=True)
    return (grad_dir - unit_rows * radial) * inv_norm


def pair_terms(img_b, txt_blk, temp_scale, logit_bias, label_signs):
    sim_vals = jnp.einsum('id,jd->ij', img_b, txt_blk, preferred_element_type=jnp.float32)
    logits = temp_scale * sim_vals + logit_bias
    weights = -label_signs * jax.nn.sigmoid(-label_signs * logits)
    weights_b = weights.astype(jnp.bfloat16)
    img_part = jnp.einsum('ij,jd->id', weights_b, txt_blk, preferred_element_type=jnp.float32)
    txt_part = jnp.einsum('ij,id->jd', weights_b, img_b, preferred_element_type=jnp.float32)
    stat_sums = jnp.stack([
        jnp.sum(jax.nn.softplus(-label_signs * logits)),
        jnp.sum(weights),
        jnp.sum(weights * sim_vals),
    ])
    return img_part, txt_part, stat_sums


def solution(mesh):
    group_size = mesh.shape['dp']
    shift_pairs = [(src_dev, (src_dev + 1) % group_size) for src_dev in range(group_size)]

    def local_fn(img_emb, txt_emb, log_temp, logit_bias):
        rows_dev = img_emb.shape[0]
        total_rows = rows_dev * group_size
        img_unit, img_inv = normalize_rows(img_emb)
        txt_unit, txt_inv = normalize_rows(txt_emb)
        img_b = img_unit.astype(jnp.bfloat16)
        txt_b = txt_unit.astype(jnp.bfloat16)
        temp_scale = jnp.exp(log_temp)
        local_ids = jnp.arange(rows_dev)
        diag_signs = jnp.where(local_ids[:, None] == local_ids[None, :], 1.0, -1.0)
        img_acc, txt_acc, stat_sums = pair_terms(img_b, txt_b, temp_scale, logit_bias, diag_signs)

        def visit_step(step_idx, loop_state):
            txt_blk, txt_acc, img_acc, stat_sums = loop_state
            txt_blk = lax.ppermute(txt_blk, 'dp', shift_pairs)
            txt_acc = lax.ppermute(txt_acc, 'dp', shift_pairs)
            img_part, txt_part, new_sums = pair_terms(img_b, txt_blk, temp_scale, logit_bias, -1.0)
            return txt_blk, txt_acc + txt_part, img_acc + img_part, stat_sums + new_sums

        loop_state = lax.fori_loop(0, group_size - 1, visit_step, (txt_b, txt_acc, img_acc, stat_sums))
        txt_acc = lax.ppermute(loop_state[1], 'dp', shift_pairs)
        img_acc = loop_state[2]
        stat_sums = lax.psum(loop_state[3], 'dp') / total_rows
        grad_img = project_back(img_unit, img_inv, temp_scale * img_acc)
        grad_txt = project_back(txt_unit, txt_inv, temp_scale * txt_acc)
        return stat_sums[0], grad_img, grad_txt, temp_scale * stat_sums[2], stat_sums[1]

    return jax.shard_map(
        local_fn,
        mesh=mesh,
        in_specs=(P('dp', None), P('dp', None), P(), P()),
        out_specs=(P(), P('dp', None), P('dp', None), P(), P()),
        check_vma=False,
    )
```

profile of v0, /device:TPU:0, one launch (start us, length us, event | category | flops | bytes accessed | tf_op | source)
XLA Modules:
  0.0 1306.1 jit_solution(17234680977413877942)
XLA Ops:
  12.5 26.5 %fusion.12 = (f32[]{:T(128)}, f32[]{:T(128)}, f32[]{:T(128)}, bf16[2048,2048]{1,0:T(8,128)(2,1)S(1)}) fusion(f32[]{:T(128)S(6)} %copy.26, f32[]{:T(128)} %exp.16, bf16[2048,1024]{1,0:T(8,128)(2,1)S(1)} %get-tuple-element.148, bf16[2048,1024]{1,0:T(8,128)(2,1)S(1)} %get-tuple-element.143), kind=kOutput, calls=%fused_computation.14 | convolution fusion | flops 8678014976 | bytes 16777236 | tf_op jit(solution)/shard_map/id,jd->ij/dot_general | solution.py:19
  63.6 1103.8 %while.16 = (s32[]{:T(128)}, bf16[2048,1024]{1,0:T(8,128)(2,1)}, f32[2048,1024]{1,0:T(8,128)}, f32[2048,1024]{1,0:T(8,128)}, f32[3]{0:T(128)S(1)}, /*index=5*/f3...) while((s32[]{:T(128)}, bf16[2048,1024]{1,0:T(8,128)(2,1)}, f32[2048,1024]{1,0:T(8,128)}, ...), condition=%wide.region_9.10_spmd, body=%wide.region_5.9_spmd.sunk | while | flops 25887244288 | bytes 234881392 | solution.py:56
  79.9 46.8 %collective-permute-done = bf16[2048,1024]{1,0:T(8,128)(2,1)} collective-permute-done((bf16[2048,1024]{1,0:T(8,128)(2,1)}, bf16[2048,1024]{1,0:T(8,128)(2,1)}, u32[]{:S(2)}, u32[]{:S(2)}) %collective-permute-start) | collective-permute-done | bytes 4194336 | tf_op jit(solution)/shard_map/while/body/eval_jaxpr/ppermute | solution.py:51
  131.5 28.1 %fusion.57 = (f32[]{:T(128)}, f32[]{:T(128)}, f32[]{:T(128)}, f32[2048,2048]{1,0:T(8,128)}) fusion(f32[]{:T(128)} %get-tuple-element.167, f32[]{:T(128)} %get-tuple-element.165, bf16[2048,1024]{1,0:T(8,128)(2,1)S(1)} %copy-done.5, bf16[2048,1024]{1,0:T(8,128)(2,1)} %collective-permute-done), kind=kOutput, calls=%fused_computation.1.clone.1 | convolution fusion | flops 8652849152 | bytes 25165844 | tf_op jit(solution)/shard_map/while/body/eval_jaxpr/id,jd->ij/dot_general | solution.py:19
  161.6 14.5 %fusion.59 = f32[2048,1024]{1,0:T(8,128)S(1)} fusion(f32[2048,1024]{1,0:T(8,128)S(1)} %bitcast.34, bf16[2048,1024]{1,0:T(8,128)(2,1)} %collective-permute-done, f32[2048,2048]{1,0:T(8,128)} %get-tuple-element.138, f32[]{:T(128)} %get-tuple-element.167, f32[]{:T(128)} %get-tuple-element.165), kind=kOutput, calls=%fused_computation.10.clone.1 | convolution fusion | flops 8617197568 | bytes 37748744 | tf_op jit(solution)/shard_map/while/body/eval_jaxpr/ij,jd->id/dot_general | solution.py:23
  176.1 40.4 %collective-permute-done.1 = f32[2048,1024]{1,0:T(8,128)} collective-permute-done((f32[2048,1024]{1,0:T(8,128)}, f32[2048,1024]{1,0:T(8,128)}, u32[]{:S(2)}, u32[]{:S(2)}) %collective-permute-start.1) | collective-permute-done | bytes 8388640 | tf_op jit(solution)/shard_map/while/body/eval_jaxpr/ppermute | solution.py:52
  216.5 16.7 %fusion.58 = f32[2048,1024]{1,0:T(8,128)} fusion(f32[2048,1024]{1,0:T(8,128)} %collective-permute-done.1, bf16[2048,1024]{1,0:T(8,128)(2,1)S(1)} %copy-done.5, f32[2048,2048]{1,0:T(8,128)} %get-tuple-element.138, f32[]{:T(128)} %get-tuple-element.167, f32[]{:T(128)} %get-tuple-element.165), kind=kOutput, calls=%fused_computation.9.clone.1 | convolution fusion | flops 8617197568 | bytes 37748744 | tf_op jit(solution)/shard_map/while/body/eval_jaxpr/ij,id->jd/dot_general | solution.py:24
  234.7 47.7 %collective-permute-done = bf16[2048,1024]{1,0:T(8,128)(2,1)} collective-permute-done((bf16[2048,1024]{1,0:T(8,128)(2,1)}, bf16[2048,1024]{1,0:T(8,128)(2,1)}, u32[]{:S(2)}, u32[]{:S(2)}) %collective-permute-start) | collective-permute-done | bytes 4194336 | tf_op jit(solution)/shard_map/while/body/eval_jaxpr/ppermute | solution.py:51
  287.2 28.1 %fusion.57 = (f32[]{:T(128)}, f32[]{:T(128)}, f32[]{:T(128)}, f32[2048,2048]{1,0:T(8,128)}) fusion(f32[]{:T(128)} %get-tuple-element.167, f32[]{:T(128)} %get-tuple-element.165, bf16[2048,1024]{1,0:T(8,128)(2,1)S(1)} %copy-done.5, bf16[2048,1024]{1,0:T(8,128)(2,1)} %collective-permute-done), kind=kOutput, calls=%fused_computation.1.clone.1 | convolution fusion | flops 8652849152 | bytes 25165844 | tf_op jit(solution)/shard_map/while/body/eval_jaxpr/id,jd->ij/dot_general | solution.py:19
  331.8 40.4 %collective-permute-done.1 = f32[2048,1024]{1,0:T(8,128)} collective-permute-done((f32[2048,1024]{1,0:T(8,128)}, f32[2048,1024]{1,0:T(8,128)}, u32[]{:S(2)}, u32[]{:S(2)}) %collective-permute-start.1) | collective-permute-done | bytes 8388640 | tf_op jit(solution)/shard_map/while/body/eval_jaxpr/ppermute | solution.py:52
  372.2 16.7 %fusion.58 = f32[2048,1024]{1,0:T(8,128)} fusion(f32[2048,1024]{1,0:T(8,128)} %collective-permute-done.1, bf16[2048,1024]{1,0:T(8,128)(2,1)S(1)} %copy-done.5, f32[2048,2048]{1,0:T(8,128)} %get-tuple-element.138, f32[]{:T(128)} %get-tuple-element.167, f32[]{:T(128)} %get-tuple-element.165), kind=kOutput, calls=%fused_computation.9.clone.1 | convolution fusion | flops 8617197568 | bytes 37748744 | tf_op jit(solution)/shard_map/while/body/eval_jaxpr/ij,id->jd/dot_general | solution.py:24
  389.5 48.6 %collective-permute-done = bf16[2048,1024]{1,0:T(8,128)(2,1)} collective-permute-done((bf16[2048,1024]{1,0:T(8,128)(2,1)}, bf16[2048,1024]{1,0:T(8,128)(2,1)}, u32[]{:S(2)}, u32[]{:S(2)}) %collective-permute-start) | collective-permute-done | bytes 4194336 | tf_op jit(solution)/shard_map/while/body/eval_jaxpr/ppermute | solution.py:51
  442.9 28.1 %fusion.57 = (f32[]{:T(128)}, f32[]{:T(128)}, f32[]{:T(128)}, f32[2048,2048]{1,0:T(8,128)}) fusion(f32[]{:T(128)} %get-tuple-element.167, f32[]{:T(128)} %get-tuple-element.165, bf16[2048,1024]{1,0:T(8,128)(2,1)S(1)} %copy-done.5, bf16[2048,1024]{1,0:T(8,128)(2,1)} %collective-permute-done), kind=kOutput, calls=%fused_computation.1.clone.1 | convolution fusion | flops 8652849152 | bytes 25165844 | tf_op jit(solution)/shard_map/while/body/eval_jaxpr/id,jd->ij/dot_general | solution.py:19
  487.5 40.4 %collective-permute-done.1 = f32[2048,1024]{1,0:T(8,128)} collective-permute-done((f32[2048,1024]{1,0:T(8,128)}, f32[2048,1024]{1,0:T(8,128)}, u32[]{:S(2)}, u32[]{:S(2)}) %collective-permute-start.1) | collective-permute-done | bytes 8388640 | tf_op jit(solution)/shard_map/while/body/eval_jaxpr/ppermute | solution.py:52
  527.9 16.7 %fusion.58 = f32[2048,1024]{1,0:T(8,128)} fusion(f32[2048,1024]{1,0:T(8,128)} %collective-permute-done.1, bf16[2048,1024]{1,0:T(8,128)(2,1)S(1)} %copy-done.5, f32[2048,2048]{1,0:T(8,128)} %get-tuple-element.138, f32[]{:T(128)} %get-tuple-element.167, f32[]{:T(128)} %get-tuple-element.165), kind=kOutput, calls=%fused_computation.9.clone.1 | convolution fusion | flops 8617197568 | bytes 37748744 | tf_op jit(solution)/shard_map/while/body/eval_jaxpr/ij,id->jd/dot_general | solution.py:24
  544.7 49.1 %collective-permute-done = bf16[2048,1024]{1,0:T(8,128)(2,1)} collective-permute-done((bf16[2048,1024]{1,0:T(8,128)(2,1)}, bf16[2048,1024]{1,0:T(8,128)(2,1)}, u32[]{:S(2)}, u32[]{:S(2)}) %collective-permute-start) | collective-permute-done | bytes 4194336 | tf_op jit(solution)/shard_map/while/body/eval_jaxpr/ppermute | solution.py:51
  598.6 28.1 %fusion.57 = (f32[]{:T(128)}, f32[]{:T(128)}, f32[]{:T(128)}, f32[2048,2048]{1,0:T(8,128)}) fusion(f32[]{:T(128)} %get-tuple-element.167, f32[]{:T(128)} %get-tuple-element.165, bf16[2048,1024]{1,0:T(8,128)(2,1)S(1)} %copy-done.5, bf16[2048,1024]{1,0:T(8,128)(2,1)} %collective-permute-done), kind=kOutput, calls=%fused_computation.1.clone.1 | convolution fusion | flops 8652849152 | bytes 25165844 | tf_op jit(solution)/shard_map/while/body/eval_jaxpr/id,jd->ij/dot_general | solution.py:19
  643.2 40.4 %collective-permute-done.1 = f32[2048,1024]{1,0:T(8,128)} collective-permute-done((f32[2048,1024]{1,0:T(8,128)}, f32[2048,1024]{1,0:T(8,128)}, u32[]{:S(2)}, u32[]{:S(2)}) %collective-permute-start.1) | collective-permute-done | bytes 8388640 | tf_op jit(solution)/shard_map/while/body/eval_jaxpr/ppermute | solution.py:52
  683.6 16.7 %fusion.58 = f32[2048,1024]{1,0:T(8,128)} fusion(f32[2048,1024]{1,0:T(8,128)} %collective-permute-done.1, bf16[2048,1024]{1,0:T(8,128)(2,1)S(1)} %copy-done.5, f32[2048,2048]{1,0:T(8,128)} %get-tuple-element.138, f32[]{:T(128)} %get-tuple-element.167, f32[]{:T(128)} %get-tuple-element.165), kind=kOutput, calls=%fused_computation.9.clone.1 | convolution fusion | flops 8617197568 | bytes 37748744 | tf_op jit(solution)/shard_map/while/body/eval_jaxpr/ij,id->jd/dot_general | solution.py:24
  700.4 49.1 %collective-permute-done = bf16[2048,1024]{1,0:T(8,128)(2,1)} collective-permute-done((bf16[2048,1024]{1,0:T(8,128)(2,1)}, bf16[2048,1024]{1,0:T(8,128)(2,1)}, u32[]{:S(2)}, u32[]{:S(2)}) %collective-permute-start) | collective-permute-done | bytes 4194336 | tf_op jit(solution)/shard_map/while/body/eval_jaxpr/ppermute | solution.py:51
  754.3 28.1 %fusion.57 = (f32[]{:T(128)}, f32[]{:T(128)}, f32[]{:T(128)}, f32[2048,2048]{1,0:T(8,128)}) fusion(f32[]{:T(128)} %get-tuple-element.167, f32[]{:T(128)} %get-tuple-element.165, bf16[2048,1024]{1,0:T(8,128)(2,1)S(1)} %copy-done.5, bf16[2048,1024]{1,0:T(8,128)(2,1)} %collective-permute-done), kind=kOutput, calls=%fused_computation.1.clone.1 | convolution fusion | flops 8652849152 | bytes 25165844 | tf_op jit(solution)/shard_map/while/body/eval_jaxpr/id,jd->ij/dot_general | solution.py:19
  798.9 40.4 %collective-permute-done.1 = f32[2048,1024]{1,0:T(8,128)} collective-permute-done((f32[2048,1024]{1,0:T(8,128)}, f32[2048,1024]{1,0:T(8,128)}, u32[]{:S(2)}, u32[]{:S(2)}) %collective-permute-start.1) | collective-permute-done | bytes 8388640 | tf_op jit(solution)/shard_map/while/body/eval_jaxpr/ppermute | solution.py:52
  839.3 16.7 %fusion.58 = f32[2048,1024]{1,0:T(8,128)} fusion(f32[2048,1024]{1,0:T(8,128)} %collective-permute-done.1, bf16[2048,1024]{1,0:T(8,128)(2,1)S(1)} %copy-done.5, f32[2048,2048]{1,0:T(8,128)} %get-tuple-element.138, f32[]{:T(128)} %get-tuple-element.167, f32[]{:T(128)} %get-tuple-element.165), kind=kOutput, calls=%fused_computation.9.clone.1 | convolution fusion | flops 8617197568 | bytes 37748744 | tf_op jit(solution)/shard_map/while/body/eval_jaxpr/ij,id->jd/dot_general | solution.py:24
  856.1 49.1 %collective-permute-done = bf16[2048,1024]{1,0:T(8,128)(2,1)} collective-permute-done((bf16[2048,1024]{1,0:T(8,128)(2,1)}, bf16[2048,1024]{1,0:T(8,128)(2,1)}, u32[]{:S(2)}, u32[]{:S(2)}) %collective-permute-start) | collective-permute-done | bytes 4194336 | tf_op jit(solution)/shard_map/while/body/eval_jaxpr/ppermute | solution.py:51
  910.0 28.1 %fusion.57 = (f32[]{:T(128)}, f32[]{:T(128)}, f32[]{:T(128)}, f32[2048,2048]{1,0:T(8,128)}) fusion(f32[]{:T(128)} %get-tuple-element.167, f32[]{:T(128)} %get-tuple-element.165, bf16[2048,1024]{1,0:T(8,128)(2,1)S(1)} %copy-done.5, bf16[2048,1024]{1,0:T(8,128)(2,1)} %collective-permute-done), kind=kOutput, calls=%fused_computation.1.clone.1 | convolution fusion | flops 8652849152 | bytes 25165844 | tf_op jit(solution)/shard_map/while/body/eval_jaxpr/id,jd->ij/dot_general | solution.py:19
  954.6 40.4 %collective-permute-done.1 = f32[2048,1024]{1,0:T(8,128)} collective-permute-done((f32[2048,1024]{1,0:T(8,128)}, f32[2048,1024]{1,0:T(8,128)}, u32[]{:S(2)}, u32[]{:S(2)}) %collective-permute-start.1) | collective-permute-done | bytes 8388640 | tf_op jit(solution)/shard_map/while/body/eval_jaxpr/ppermute | solution.py:52
  995.0 16.7 %fusion.58 = f32[2048,1024]{1,0:T(8,128)} fusion(f32[2048,1024]{1,0:T(8,128)} %collective-permute-done.1, bf16[2048,1024]{1,0:T(8,128)(2,1)S(1)} %copy-done.5, f32[2048,2048]{1,0:T(8,128)} %get-tuple-element.138, f32[]{:T(128)} %get-tuple-element.167, f32[]{:T(128)} %get-tuple-element.165), kind=kOutput, calls=%fused_computation.9.clone.1 | convolution fusion | flops 8617197568 | bytes 37748744 | tf_op jit(solution)/shard_map/while/body/eval_jaxpr/ij,id->jd/dot_general | solution.py:24
  1011.8 49.1 %collective-permute-done = bf16[2048,1024]{1,0:T(8,128)(2,1)} collective-permute-done((bf16[2048,1024]{1,0:T(8,128)(2,1)}, bf16[2048,1024]{1,0:T(8,128)(2,1)}, u32[]{:S(2)}, u32[]{:S(2)}) %collective-permute-start) | collective-permute-done | bytes 4194336 | tf_op jit(solution)/shard_map/while/body/eval_jaxpr/ppermute | solution.py:51
  1065.7 28.1 %fusion.57 = (f32[]{:T(128)}, f32[]{:T(128)}, f32[]{:T(128)}, f32[2048,2048]{1,0:T(8,128)}) fusion(f32[]{:T(128)} %get-tuple-element.167, f32[]{:T(128)} %get-tuple-element.165, bf16[2048,1024]{1,0:T(8,128)(2,1)S(1)} %copy-done.5, bf16[2048,1024]{1,0:T(8,128)(2,1)} %collective-permute-done), kind=kOutput, calls=%fused_computation.1.clone.1 | convolution fusion | flops 8652849152 | bytes 25165844 | tf_op jit(solution)/shard_map/while/body/eval_jaxpr/id,jd->ij/dot_general | solution.py:19
  1110.3 40.4 %collective-permute-done.1 = f32[2048,1024]{1,0:T(8,128)} collective-permute-done((f32[2048,1024]{1,0:T(8,128)}, f32[2048,1024]{1,0:T(8,128)}, u32[]{:S(2)}, u32[]{:S(2)}) %collective-permute-start.1) | collective-permute-done | bytes 8388640 | tf_op jit(solution)/shard_map/while/body/eval_jaxpr/ppermute | solution.py:52
  1150.7 16.7 %fusion.58 = f32[2048,1024]{1,0:T(8,128)} fusion(f32[2048,1024]{1,0:T(8,128)} %collective-permute-done.1, bf16[2048,1024]{1,0:T(8,128)(2,1)S(1)} %copy-done.5, f32[2048,2048]{1,0:T(8,128)} %get-tuple-element.138, f32[]{:T(128)} %get-tuple-element.167, f32[]{:T(128)} %get-tuple-element.165), kind=kOutput, calls=%fused_computation.9.clone.1 | convolution fusion | flops 8617197568 | bytes 37748744 | tf_op jit(solution)/shard_map/while/body/eval_jaxpr/ij,id->jd/dot_general | solution.py:24
  1167.4 112.4 %psum.7 = f32[3]{0:T(128)S(1)} all-reduce(f32[3]{0:T(128)S(1)} %get-tuple-element.49), channel_id=1, replica_groups=mesh['dp'=8] {'dp'}, use_global_device_ids=true, to_apply=%region_10.11 | all-reduce | flops 3 | bytes 24 | tf_op jit(solution)/shard_map/psum | solution.py:59
  (131 shorter events, 199.4 us)
Async XLA Ops:
  12.5 37.5 %copy-start.4 = (bf16[2048,1024]{1,0:T(8,128)(2,1)}, bf16[2048,1024]{1,0:T(8,128)(2,1)S(1)}, u32[]{:S(2)}) copy-start(bf16[2048,1024]{1,0:T(8,128)(2,1)S(1)} %get-tuple-element.148) | copy-start | bytes 12582916
  63.6 1217.5 %copy-start.10 = (f32[2048]{0:T(1024)S(1)}, f32[2048]{0:T(1024)}, u32[]{:S(2)}) copy-start(f32[2048]{0:T(1024)} %copy-done.9) | copy-start | bytes 24580
  76.4 50.2 %collective-permute-start = (bf16[2048,1024]{1,0:T(8,128)(2,1)}, bf16[2048,1024]{1,0:T(8,128)(2,1)}, u32[]{:S(2)}, u32[]{:S(2)}) collective-permute-start(bf16[2048,1024]{1,0:T(8,128)(2,1)} %get-tuple-element.152), channel_id=1, source_target_pairs={{0,1},{1,2},{2,3},{3,4},{4,5},{5,6},{6,7},{7,0}} | collective-permute-start | bytes 12582920 | tf_op jit(solution)/shard_map/while/body/eval_jaxpr/ppermute | solution.py:51
  77.3 139.3 %collective-permute-start.1 = (f32[2048,1024]{1,0:T(8,128)}, f32[2048,1024]{1,0:T(8,128)}, u32[]{:S(2)}, u32[]{:S(2)}) collective-permute-start(f32[2048,1024]{1,0:T(8,128)} %get-tuple-element.153), channel_id=1, source_target_pairs={{0,1},{1,2},{2,3},{3,4},{4,5},{5,6},{6,7},{7,0}} | collective-permute-start | bytes 25165832 | tf_op jit(solution)/shard_map/while/body/eval_jaxpr/ppermute | solution.py:52
  79.9 51.6 %copy-start.5 = (bf16[2048,1024]{1,0:T(8,128)(2,1)S(1)}, bf16[2048,1024]{1,0:T(8,128)(2,1)}, u32[]{:S(2)}) copy-start(bf16[2048,1024]{1,0:T(8,128)(2,1)} %get-tuple-element.166) | copy-start | bytes 12582916 | tf_op jit(solution)/shard_map/while
  126.7 34.9 %slice-start = ((s8[8388608]{0:T(1024)(128)(4,1)}), s8[4194304]{0:T(1024)(128)(4,1)S(1)}, s32[]{:S(2)}) async-start(s8[8388608]{0:T(1024)(128)(4,1)} %bitcast.33), calls=%async_computation | async-start | bytes 8388608 | tf_op jit(solution)/shard_map/while
  176.1 57.1 %copy-start.2 = (f32[2048,1024]{1,0:T(8,128)}, f32[2048,1024]{1,0:T(8,128)S(1)}, u32[]{:S(2)}) copy-start(f32[2048,1024]{1,0:T(8,128)S(1)} %fusion.59) | copy-start | bytes 25165828 | tf_op jit(solution)/shard_map/while
  233.2 49.1 %collective-permute-start = (bf16[2048,1024]{1,0:T(8,128)(2,1)}, bf16[2048,1024]{1,0:T(8,128)(2,1)}, u32[]{:S(2)}, u32[]{:S(2)}) collective-permute-start(bf16[2048,1024]{1,0:T(8,128)(2,1)} %get-tuple-element.152), channel_id=1, source_target_pairs={{0,1},{1,2},{2,3},{3,4},{4,5},{5,6},{6,7},{7,0}} | collective-permute-start | bytes 12582920 | tf_op jit(solution)/shard_map/while/body/eval_jaxpr/ppermute | solution.py:51
  233.2 139.0 %collective-permute-start.1 = (f32[2048,1024]{1,0:T(8,128)}, f32[2048,1024]{1,0:T(8,128)}, u32[]{:S(2)}, u32[]{:S(2)}) collective-permute-start(f32[2048,1024]{1,0:T(8,128)} %get-tuple-element.153), channel_id=1, source_target_pairs={{0,1},{1,2},{2,3},{3,4},{4,5},{5,6},{6,7},{7,0}} | collective-permute-start | bytes 25165832 | tf_op jit(solution)/shard_map/while/body/eval_jaxpr/ppermute | solution.py:52
  234.7 52.5 %copy-start.5 = (bf16[2048,1024]{1,0:T(8,128)(2,1)S(1)}, bf16[2048,1024]{1,0:T(8,128)(2,1)}, u32[]{:S(2)}) copy-start(bf16[2048,1024]{1,0:T(8,128)(2,1)} %get-tuple-element.166) | copy-start | bytes 12582916 | tf_op jit(solution)/shard_map/while
  331.8 57.1 %copy-start.2 = (f32[2048,1024]{1,0:T(8,128)}, f32[2048,1024]{1,0:T(8,128)S(1)}, u32[]{:S(2)}) copy-start(f32[2048,1024]{1,0:T(8,128)S(1)} %fusion.59) | copy-start | bytes 25165828 | tf_op jit(solution)/shard_map/while
  388.9 49.1 %collective-permute-start = (bf16[2048,1024]{1,0:T(8,128)(2,1)}, bf16[2048,1024]{1,0:T(8,128)(2,1)}, u32[]{:S(2)}, u32[]{:S(2)}) collective-permute-start(bf16[2048,1024]{1,0:T(8,128)(2,1)} %get-tuple-element.152), channel_id=1, source_target_pairs={{0,1},{1,2},{2,3},{3,4},{4,5},{5,6},{6,7},{7,0}} | collective-permute-start | bytes 12582920 | tf_op jit(solution)/shard_map/while/body/eval_jaxpr/ppermute | solution.py:51
  388.9 139.0 %collective-permute-start.1 = (f32[2048,1024]{1,0:T(8,128)}, f32[2048,1024]{1,0:T(8,128)}, u32[]{:S(2)}, u32[]{:S(2)}) collective-permute-start(f32[2048,1024]{1,0:T(8,128)} %get-tuple-element.153), channel_id=1, source_target_pairs={{0,1},{1,2},{2,3},{3,4},{4,5},{5,6},{6,7},{7,0}} | collective-permute-start | bytes 25165832 | tf_op jit(solution)/shard_map/while/body/eval_jaxpr/ppermute | solution.py:52
  389.5 53.4 %copy-start.5 = (bf16[2048,1024]{1,0:T(8,128)(2,1)S(1)}, bf16[2048,1024]{1,0:T(8,128)(2,1)}, u32[]{:S(2)}) copy-start(bf16[2048,1024]{1,0:T(8,128)(2,1)} %get-tuple-element.166) | copy-start | bytes 12582916 | tf_op jit(solution)/shard_map/while
  487.5 57.1 %copy-start.2 = (f32[2048,1024]{1,0:T(8,128)}, f32[2048,1024]{1,0:T(8,128)S(1)}, u32[]{:S(2)}) copy-start(f32[2048,1024]{1,0:T(8,128)S(1)} %fusion.59) | copy-start | bytes 25165828 | tf_op jit(solution)/shard_map/while
  544.6 49.1 %collective-permute-start = (bf16[2048,1024]{1,0:T(8,128)(2,1)}, bf16[2048,1024]{1,0:T(8,128)(2,1)}, u32[]{:S(2)}, u32[]{:S(2)}) collective-permute-start(bf16[2048,1024]{1,0:T(8,128)(2,1)} %get-tuple-element.152), channel_id=1, source_target_pairs={{0,1},{1,2},{2,3},{3,4},{4,5},{5,6},{6,7},{7,0}} | collective-permute-start | bytes 12582920 | tf_op jit(solution)/shard_map/while/body/eval_jaxpr/ppermute | solution.py:51
  544.6 139.0 %collective-permute-start.1 = (f32[2048,1024]{1,0:T(8,128)}, f32[2048,1024]{1,0:T(8,128)}, u32[]{:S(2)}, u32[]{:S(2)}) collective-permute-start(f32[2048,1024]{1,0:T(8,128)} %get-tuple-element.153), channel_id=1, source_target_pairs={{0,1},{1,2},{2,3},{3,4},{4,5},{5,6},{6,7},{7,0}} | collective-permute-start | bytes 25165832 | tf_op jit(solution)/shard_map/while/body/eval_jaxpr/ppermute | solution.py:52
  544.6 54.0 %copy-start.5 = (bf16[2048,1024]{1,0:T(8,128)(2,1)S(1)}, bf16[2048,1024]{1,0:T(8,128)(2,1)}, u32[]{:S(2)}) copy-start(bf16[2048,1024]{1,0:T(8,128)(2,1)} %get-tuple-element.166) | copy-start | bytes 12582916 | tf_op jit(solution)/shard_map/while
  643.2 57.1 %copy-start.2 = (f32[2048,1024]{1,0:T(8,128)}, f32[2048,1024]{1,0:T(8,128)S(1)}, u32[]{:S(2)}) copy-start(f32[2048,1024]{1,0:T(8,128)S(1)} %fusion.59) | copy-start | bytes 25165828 | tf_op jit(solution)/shard_map/while
  700.3 49.1 %collective-permute-start = (bf16[2048,1024]{1,0:T(8,128)(2,1)}, bf16[2048,1024]{1,0:T(8,128)(2,1)}, u32[]{:S(2)}, u32[]{:S(2)}) collective-permute-start(bf16[2048,1024]{1,0:T(8,128)(2,1)} %get-tuple-element.152), channel_id=1, source_target_pairs={{0,1},{1,2},{2,3},{3,4},{4,5},{5,6},{6,7},{7,0}} | collective-permute-start | bytes 12582920 | tf_op jit(solution)/shard_map/while/body/eval_jaxpr/ppermute | solution.py:51
  700.3 139.0 %collective-permute-start.1 = (f32[2048,1024]{1,0:T(8,128)}, f32[2048,1024]{1,0:T(8,128)}, u32[]{:S(2)}, u32[]{:S(2)}) collective-permute-start(f32[2048,1024]{1,0:T(8,128)} %get-tuple-element.153), channel_id=1, source_target_pairs={{0,1},{1,2},{2,3},{3,4},{4,5},{5,6},{6,7},{7,0}} | collective-permute-start | bytes 25165832 | tf_op jit(solution)/shard_map/while/body/eval_jaxpr/ppermute | solution.py:52
  700.3 54.0 %copy-start.5 = (bf16[2048,1024]{1,0:T(8,128)(2,1)S(1)}, bf16[2048,1024]{1,0:T(8,128)(2,1)}, u32[]{:S(2)}) copy-start(bf16[2048,1024]{1,0:T(8,128)(2,1)} %get-tuple-element.166) | copy-start | bytes 12582916 | tf_op jit(solution)/shard_map/while
  798.9 57.1 %copy-start.2 = (f32[2048,1024]{1,0:T(8,128)}, f32[2048,1024]{1,0:T(8,128)S(1)}, u32[]{:S(2)}) copy-start(f32[2048,1024]{1,0:T(8,128)S(1)} %fusion.59) | copy-start | bytes 25165828 | tf_op jit(solution)/shard_map/while
  856.0 49.1 %collective-permute-start = (bf16[2048,1024]{1,0:T(8,128)(2,1)}, bf16[2048,1024]{1,0:T(8,128)(2,1)}, u32[]{:S(2)}, u32[]{:S(2)}) collective-permute-start(bf16[2048,1024]{1,0:T(8,128)(2,1)} %get-tuple-element.152), channel_id=1, source_target_pairs={{0,1},{1,2},{2,3},{3,4},{4,5},{5,6},{6,7},{7,0}} | collective-permute-start | bytes 12582920 | tf_op jit(solution)/shard_map/while/body/eval_jaxpr/ppermute | solution.py:51
  856.0 139.0 %collective-permute-start.1 = (f32[2048,1024]{1,0:T(8,128)}, f32[2048,1024]{1,0:T(8,128)}, u32[]{:S(2)}, u32[]{:S(2)}) collective-permute-start(f32[2048,1024]{1,0:T(8,128)} %get-tuple-element.153), channel_id=1, source_target_pairs={{0,1},{1,2},{2,3},{3,4},{4,5},{5,6},{6,7},{7,0}} | collective-permute-start | bytes 25165832 | tf_op jit(solution)/shard_map/while/body/eval_jaxpr/ppermute | solution.py:52
  856.0 54.0 %copy-start.5 = (bf16[2048,1024]{1,0:T(8,128)(2,1)S(1)}, bf16[2048,1024]{1,0:T(8,128)(2,1)}, u32[]{:S(2)}) copy-start(bf16[2048,1024]{1,0:T(8,128)(2,1)} %get-tuple-element.166) | copy-start | bytes 12582916 | tf_op jit(solution)/shard_map/while
  954.6 57.1 %copy-start.2 = (f32[2048,1024]{1,0:T(8,128)}, f32[2048,1024]{1,0:T(8,128)S(1)}, u32[]{:S(2)}) copy-start(f32[2048,1024]{1,0:T(8,128)S(1)} %fusion.59) | copy-start | bytes 25165828 | tf_op jit(solution)/shard_map/while
  1011.7 49.1 %collective-permute-start = (bf16[2048,1024]{1,0:T(8,128)(2,1)}, bf16[2048,1024]{1,0:T(8,128)(2,1)}, u32[]{:S(2)}, u32[]{:S(2)}) collective-permute-start(bf16[2048,1024]{1,0:T(8,128)(2,1)} %get-tuple-element.152), channel_id=1, source_target_pairs={{0,1},{1,2},{2,3},{3,4},{4,5},{5,6},{6,7},{7,0}} | collective-permute-start | bytes 12582920 | tf_op jit(solution)/shard_map/while/body/eval_jaxpr/ppermute | solution.py:51
  1011.7 139.0 %collective-permute-start.1 = (f32[2048,1024]{1,0:T(8,128)}, f32[2048,1024]{1,0:T(8,128)}, u32[]{:S(2)}, u32[]{:S(2)}) collective-permute-start(f32[2048,1024]{1,0:T(8,128)} %get-tuple-element.153), channel_id=1, source_target_pairs={{0,1},{1,2},{2,3},{3,4},{4,5},{5,6},{6,7},{7,0}} | collective-permute-start | bytes 25165832 | tf_op jit(solution)/shard_map/while/body/eval_jaxpr/ppermute | solution.py:52
  1011.7 54.0 %copy-start.5 = (bf16[2048,1024]{1,0:T(8,128)(2,1)S(1)}, bf16[2048,1024]{1,0:T(8,128)(2,1)}, u32[]{:S(2)}) copy-start(bf16[2048,1024]{1,0:T(8,128)(2,1)} %get-tuple-element.166) | copy-start | bytes 12582916 | tf_op jit(solution)/shard_map/while
  1110.3 57.1 %copy-start.2 = (f32[2048,1024]{1,0:T(8,128)}, f32[2048,1024]{1,0:T(8,128)S(1)}, u32[]{:S(2)}) copy-start(f32[2048,1024]{1,0:T(8,128)S(1)} %fusion.59) | copy-start | bytes 25165828 | tf_op jit(solution)/shard_map/while
  1167.4 126.3 %collective-permute-start.2 = (f32[2048,1024]{1,0:T(8,128)}, f32[2048,1024]{1,0:T(8,128)}, u32[]{:S(2)}, u32[]{:S(2)}) collective-permute-start(f32[2048,1024]{1,0:T(8,128)} %get-tuple-element.51), channel_id=1, source_target_pairs={{0,1},{1,2},{2,3},{3,4},{4,5},{5,6},{6,7},{7,0}} | collective-permute-start | bytes 25165832 | tf_op jit(solution)/shard_map/ppermute | solution.py:57
  (20 other events, 483.6 us)
where the time goes:
time: 1320 us; the launch traced here: 1310 us
  waiting for transfers between devices  622 us (47%)
  matrix products  464 us (35%)
  blocking collectives  112 us (8%)
  other arithmetic  46.9 us (4%)
  local copies, waits for them, and re-layouts  37.3 us (3%)
    ppermute x7, waiting for transfers between devices, visit_step(): txt_blk = lax.ppermute(txt_blk, 'dp', shift_pairs)  339 us
    ppermute x7, waiting for transfers between devices, visit_step(): txt_acc = lax.ppermute(txt_acc, 'dp', shift_pairs)  283 us
    dot_general x8, matrix products, pair_terms(): jnp.einsum('id,jd->ij', img_b, txt_blk, preferred_element_type=jnp.float32)  223 us
    dot_general x8, matrix products, pair_terms(): jnp.einsum('ij,id->jd', weights_b, img_b, preferred_element_type=jnp.floa...  128 us
    dot_general x8, matrix products, pair_terms(): jnp.einsum('ij,jd->id', weights_b, txt_blk, preferred_element_type=jnp.fl...  113 us
    psum x1, blocking collectives, local_fn(): stat_sums = lax.psum(loop_state[3], 'dp') / total_rows  112 us
    while x63, local copies, waits for them, and re-layouts  34.1 us
  transfers between devices with their start and end apart: 15, of which 14 were waited for; matrix products, arithmetic and copies ran while one was open for 27% of the time, Pallas kernels for 0%

commit v1 on v0

v1 whole, which is shorter than its diff:
```python
import functools

import jax
import jax.numpy as jnp
from jax import lax
from jax.experimental import pallas as pl
from jax.experimental.pallas import tpu as pltpu
from jax.sharding import PartitionSpec as P

TILE = 512
STRIP = 64
NT = (((1,), (1,)), ((), ()))
NN = (((1,), (0,)), ((), ()))
TN = (((0,), (0,)), ((), ()))


def dotf(a, b, dims):
    return lax.dot_general(a, b, dims, preferred_element_type=jnp.float32)


def pair_kernel(rows_i, rows_t, has_u, has_v, diag, *refs):
    n_i, n_t = len(rows_i), len(rows_t)
    refs = list(refs)

    def take(n):
        out = refs[:n]
        del refs[:n]
        return out

    (par,) = take(1)
    imgs, txts = take(n_i), take(n_t)
    u_in, v_in = take(has_u), take(has_v)
    (st_in,) = take(1)
    u_out, v_out = take(n_i), take(n_t)
    (st_out,) = take(1)
    img, txt, u_acc, v_acc, s_buf, h_buf, sem_i, sem_t, sem_u, sem_v, sem_uo, sem_vo = refs

    def tiles(arrs, rows):
        out = []
        for arr, n in zip(arrs, rows):
            out += [arr.at[pl.ds(k * TILE, TILE)] for k in range(n // TILE)]
        return out

    img_t, txt_t = tiles(imgs, rows_i), tiles(txts, rows_t)
    mi, mt = len(img_t), len(txt_t)
    at = lambda ref, k: ref.at[pl.ds(k * TILE, TILE)]
    for k in range(max(mi, mt)):
        if k < mi:
            pltpu.make_async_copy(img_t[k], at(img, k), sem_i.at[k]).start()
        if k < mt:
            pltpu.make_async_copy(txt_t[k], at(txt, k), sem_t.at[k]).start()
    v_src, u_src = tiles(v_in, rows_t), tiles(u_in, rows_i)
    nv, nu = len(v_src), len(u_src)
    for k, src in enumerate(v_src):
        pltpu.make_async_copy(src, at(v_acc, k), sem_v.at[k]).start()
    for k, src in enumerate(u_src):
        pltpu.make_async_copy(src, at(u_acc, k), sem_u.at[k]).start()

    def clear(acc, lo, hi):
        def one(k, carry):
            acc[pl.ds(pl.multiple_of(k * 64, 64), 64)] = jnp.zeros((64, acc.shape[1]), jnp.float32)
            return carry

        lax.fori_loop(lo * (TILE // 64), hi * (TILE // 64), one, 0)

    clear(v_acc, nv, mt)
    clear(u_acc, nu, mi)
    st_out[...] = st_in[...]
    ts, bias = par[0], par[1]

    def row(i, carry):
        i0 = pl.multiple_of(i * TILE, TILE)
        a_ref = img.at[pl.ds(i0, TILE)]
        u_ref = u_acc.at[pl.ds(i0, TILE)]
        pltpu.make_async_copy(img_t[0], a_ref, sem_i.at[i]).wait()
        if nu:
            @pl.when(i < nu)
            def _():
                pltpu.make_async_copy(u_ref, u_ref, sem_u.at[i]).wait()

        def col(j, carry):
            j0 = pl.multiple_of(j * TILE, TILE)
            b_ref = txt.at[pl.ds(j0, TILE)]
            v_ref = v_acc.at[pl.ds(j0, TILE)]

            @pl.when(i == 0)
            def _():
                pltpu.make_async_copy(txt_t[0], b_ref, sem_t.at[j]).wait()

            if nv:
                @pl.when(jnp.logical_and(i == 0, j < nv))
                def _():
                    pltpu.make_async_copy(v_ref, v_ref, sem_v.at[j]).wait()

            a, b = a_ref[...], b_ref[...]
            s_buf[...] = dotf(a, b, NT)
            soft = jnp.zeros((8, TILE), jnp.float32)
            wsum = jnp.zeros((8, TILE), jnp.float32)
            wsim = jnp.zeros((8, TILE), jnp.float32)
            for r in range(0, TILE, STRIP):
                s = s_buf[r:r + STRIP]
                logit = s * ts + bias
                if diag:
                    rid = lax.broadcasted_iota(jnp.int32, (STRIP, TILE), 0) + r
                    cid = lax.broadcasted_iota(jnp.int32, (STRIP, TILE), 1)
                    own = jnp.logical_and(rid == cid, i == j)
                    logit = jnp.where(own, -logit, logit)
                e = jnp.exp(jnp.minimum(logit, -logit))
                w = jnp.where(logit >= 0, 1.0, e) / (1.0 + e)
                if diag:
                    w = jnp.where(own, -w, w)
                h_buf[r:r + STRIP] = w.astype(jnp.bfloat16)
                grp = lambda x: [x[k * 8:(k + 1) * 8] for k in range(STRIP // 8)]
                prods = grp(e)
                while len(prods) > 1:
                    prods = [p + q + p * q for p, q in zip(prods[::2], prods[1::2])]
                soft = soft + jnp.log1p(prods[0])
                for x in grp(jnp.maximum(logit, 0.0)):
                    soft = soft + x
                for x in grp(w):
                    wsum = wsum + x
                for x in grp(w * s):
                    wsim = wsim + x
            st_out[0] += soft
            st_out[1] += wsum
            st_out[2] += wsim
            h = h_buf[...]
            u_ref[...] += dotf(h, b, NN)
            v_ref[...] += dotf(h, a, TN)
            return carry

        lax.fori_loop(0, mt, col, 0)
        return carry

    u_dst = tiles(u_out, rows_i)
    if len(u_out) == 1:
        def row_store(i, carry):
            row(i, carry)
            i0 = pl.multiple_of(i * TILE, TILE)
            pltpu.make_async_copy(u_acc.at[pl.ds(i0, TILE)], u_out[0].at[pl.ds(i0, TILE)], sem_uo.at[i]).start()
            return carry

        lax.fori_loop(0, mi, row_store, 0)
    else:
        lax.fori_loop(0, mi, row, 0)
        for k in range(mi):
            pltpu.make_async_copy(at(u_acc, k), u_dst[k], sem_uo.at[k]).start()
    v_dst = tiles(v_out, rows_t)
    for k in range(mt):
        pltpu.make_async_copy(at(v_acc, k), v_dst[k], sem_vo.at[k]).start()
    for k in range(mi):
        pltpu.make_async_copy(at(u_acc, k), u_dst[k], sem_uo.at[k]).wait()
    for k in range(mt):
        pltpu.make_async_copy(at(v_acc, k), v_dst[k], sem_vo.at[k]).wait()


def pair(par, imgs, txts, stats, u_in=(), v_in=(), diag=False):
    width = imgs[0].shape[1]
    rows_i = tuple(x.shape[0] for x in imgs)
    rows_t = tuple(x.shape[0] for x in txts)
    m, n = sum(rows_i), sum(rows_t)
    mi, mt = m // TILE, n // TILE
    any_spec = pl.BlockSpec(memory_space=pl.ANY)
    vmem = pl.BlockSpec(memory_space=pltpu.VMEM)
    ins = [par] + list(imgs) + list(txts)
    specs = [pl.BlockSpec(memory_space=pltpu.SMEM)] + [any_spec] * (len(imgs) + len(txts))
    aliases = {}
    u_in, v_in = list(u_in), list(v_in)
    for k in range(len(u_in)):
        aliases[len(ins) + k] = k
    ins += u_in
    for k in range(len(v_in)):
        aliases[len(ins) + k] = len(imgs) + k
    ins += v_in
    specs += [any_spec] * (len(u_in) + len(v_in))
    ins.append(stats)
    specs.append(vmem)
    f32 = lambda r: jax.ShapeDtypeStruct((r, width), jnp.float32)
    outs = [f32(r) for r in rows_i] + [f32(r) for r in rows_t] + [jax.ShapeDtypeStruct(stats.shape, stats.dtype)]
    dma = lambda k: pltpu.SemaphoreType.DMA((k,))
    call = pl.pallas_call(
        functools.partial(pair_kernel, rows_i, rows_t, len(u_in), len(v_in), diag),
        out_shape=outs,
        in_specs=specs,
        out_specs=[any_spec] * (len(imgs) + len(txts)) + [vmem],
        scratch_shapes=[
            pltpu.VMEM((m, width), jnp.bfloat16),
            pltpu.VMEM((n, width), jnp.bfloat16),
            pltpu.VMEM((m, width), jnp.float32),
            pltpu.VMEM((n, width), jnp.float32),
            pltpu.VMEM((TILE, TILE), jnp.float32),
            pltpu.VMEM((TILE, TILE), jnp.bfloat16),
            dma(mi), dma(mt), dma(mi), dma(mt), dma(mi), dma(mt),
        ],
        input_output_aliases=aliases,
        cost_estimate=pl.CostEstimate(flops=6 * m * n * width, bytes_accessed=6 * (m + n) * width, transcendentals=0),
        compiler_params=pltpu.CompilerParams(vmem_limit_bytes=62 * 1024 * 1024),
    )
    res = call(*ins)
    return res[:len(imgs)], res[len(imgs):-1], res[-1]


def normalize_rows(emb):
    emb32 = emb.astype(jnp.float32)
    inv_norm = lax.rsqrt(jnp.sum(emb32 * emb32, axis=-1, keepdims=True))
    return emb32 * inv_norm, inv_norm


def norm_bf16(emb):
    return normalize_rows(emb)[0].astype(jnp.bfloat16)


def finish_kernel(n_parts, *refs):
    ts_ref, emb_ref = refs[0], refs[1]
    parts, out_ref = refs[2:2 + n_parts], refs[-1]
    emb = emb_ref[...].astype(jnp.float32)
    inv = lax.rsqrt(jnp.sum(emb * emb, axis=-1, keepdims=True))
    unit = emb * inv
    total = parts[0][...]
    for p in parts[1:]:
        total = total + p[...]
    total = total * ts_ref[0]
    radial = jnp.sum(unit * total, axis=-1, keepdims=True)
    out_ref[...] = (total - unit * radial) * inv


def finish(par, emb, parts, chunk, rows, prev):
    width = emb.shape[1]
    step = 256
    per = rows // step
    smem = pl.BlockSpec(memory_space=pltpu.SMEM)
    blk = lambda off: pl.BlockSpec((step, width), lambda i, off=off: (i + off // step, 0))
    ins = [par, emb] + [p for p, _ in parts]
    specs = [smem, blk(chunk * rows)] + [blk(off) for _, off in parts]
    aliases = {}
    if prev is not None:
        aliases = {len(ins): 0}
        ins.append(prev)
        specs.append(pl.BlockSpec(memory_space=pl.ANY))
    return pl.pallas_call(
        functools.partial(finish_kernel, len(parts)),
        out_shape=jax.ShapeDtypeStruct(emb.shape, jnp.float32),
        grid=(per,),
        in_specs=specs,
        out_specs=blk(chunk * rows),
        input_output_aliases=aliases,
        cost_estimate=pl.CostEstimate(flops=40 * rows * width, bytes_accessed=16 * rows * width, transcendentals=0),
        compiler_params=pltpu.CompilerParams(vmem_limit_bytes=32 * 1024 * 1024),
    )(*ins)


def solution(mesh):
    size = mesh.shape['dp']

    def flip(bit):
        return [(k, k ^ bit) for k in range(size)]

    def local_fn(img_emb, txt_emb, log_temp, logit_bias):
        rows = img_emb.shape[0]
        total_rows = rows * size
        nq = 4
        q = rows // nq
        temp_scale = jnp.exp(log_temp)
        par = jnp.stack([temp_scale, logit_bias])
        SIB, XN, YN = 1, 2, 4
        cut = lambda x, k: lax.slice_in_dim(x, k * q, (k + 1) * q)

        def over(x, bit):
            return lax.ppermute(x, 'dp', flip(bit))

        xi = [over(norm_bf16(cut(img_emb, k)), XN) for k in range(nq)]
        yt = [over(norm_bf16(cut(txt_emb, k)), YN) for k in range(nq)]
        own_i, own_t = norm_bf16(img_emb), norm_bf16(txt_emb)
        sib_i = over(own_i, SIB)
        xs = [over(x, SIB) for x in xi]
        st = jnp.zeros((3, 8, TILE), jnp.float32)
        u23, vb, gx, gy = [None] * nq, [None] * nq, [None] * nq, [None] * nq

        def send_u(k):
            mine, other = u23[k]
            gx[k] = over(mine + over(other, SIB), XN)

        def send_v(k):
            gy[k] = over(vb[k], YN)

        (u0,), (va,), st = pair(par, [own_i], [own_t], st, diag=True)
        (u0, u1), (vb[0],), st = pair(par, [own_i, sib_i], [yt[0]], st, u_in=[u0])
        u23[0], (va,), st = pair(par, [xi[0], xs[0]], [own_t], st, v_in=[va])
        (u0, u1), (vb[1],), st = pair(par, [own_i, sib_i], [yt[1]], st, u_in=[u0, u1])
        u23[1], (va,), st = pair(par, [xi[1], xs[1]], [own_t], st, v_in=[va])
        u23[0], vb, st = pair(par, [xi[0], xs[0]], yt, st, u_in=u23[0], v_in=vb[:2])
        vb = list(vb)
        send_u(0)
        imgs = [xi[1], xs[1], xi[2], xs[2], xi[3], xs[3]]
        res, (vb[0],), st = pair(par, imgs, [yt[0]], st, u_in=u23[1], v_in=[vb[0]])
        u23[1], u23[2], u23[3] = res[0:2], res[2:4], res[4:6]
        send_v(0)
        u23[1], vb[1:], st = pair(par, [xi[1], xs[1]], yt[1:], st, u_in=u23[1], v_in=vb[1:])
        send_u(1)
        res, (vb[1],), st = pair(par, [xi[2], xs[2], xi[3], xs[3]], [yt[1]], st,
                                 u_in=list(u23[2]) + list(u23[3]), v_in=[vb[1]])
        u23[2], u23[3] = res[0:2], res[2:4]
        send_v(1)
        for k in (2, 3):
            u23[k], (va,), st = pair(par, [xi[k], xs[k]], [own_t], st, u_in=u23[k], v_in=[va])
            u23[k], vb[2:], st = pair(par, [xi[k], xs[k]], yt[2:], st, u_in=u23[k], v_in=vb[2:])
            send_u(k)
        for k in (2, 3):
            (u0, u1), (vb[k],), st = pair(par, [own_i, sib_i], [yt[k]], st, u_in=[u0, u1], v_in=[vb[k]])
            send_v(k)
        (u1,), (va,), st = pair(par, [sib_i], [own_t], st, u_in=[u1], v_in=[va])
        us = over(u1, SIB)
        sums = lax.psum(jnp.sum(st, axis=(1, 2)), 'dp') / total_rows
        grad_img = grad_txt = None
        for k in range(nq):
            grad_img = finish(par, img_emb, [(u0, k * q), (us, k * q), (gx[k], 0)], k, q, grad_img)
            grad_txt = finish(par, txt_emb, [(va, k * q), (gy[k], 0)], k, q, grad_txt)
        return sums[0], grad_img, grad_txt, temp_scale * sums[2], sums[1]

    return jax.shard_map(
        local_fn,
        mesh=mesh,
        in_specs=(P('dp', None), P('dp', None), P(), P()),
        out_specs=(P(), P('dp', None), P('dp', None), P(), P()),
        check_vma=False,
    )
```

time: 1320 us -> 901 us (0.68)
  Pallas kernels: 0 us -> 506 us
  matrix products: 464 us -> 0 us
  waiting for transfers between devices: 622 us -> 174 us
  blocking collectives: 112 us -> 152 us
  local copies, waits for them, and re-layouts: 37.3 us -> 11.9 us
  other arithmetic: 46.9 us -> 27.6 us
    pallas_call x0 -> x24, Pallas kernels: none -> 506 us  [the longest x16 482 us: pair(): res = call(*ins)]
    dot_general x24 -> x0, matrix products: 464 us -> none  [the longest x8 223 us: pair_terms(): jnp.einsum('id,jd->ij', img_b, txt_blk, preferred_element_type=jnp.float32)]
    ppermute x15 -> x26, waiting for transfers between devices: 622 us -> 174 us  [over(): return lax.ppermute(x, 'dp', flip(bit))]
    psum x1, blocking collectives: 112 us -> 152 us  [local_fn(): sums = lax.psum(jnp.sum(st, axis=(1, 2)), 'dp') / total_rows]
    while x63 -> x0, local copies, waits for them, and re-layouts: 34.1 us -> none
  transfers between devices with their start and end apart: 15 -> 26, of which waited for: 14 -> 6; matrix products, arithmetic and copies ran while one was open for 27% -> 3% of each run, Pallas kernels for 0% -> 25%
where the time goes in v1:
time: 901 us; the launch traced here: 892 us
  Pallas kernels  506 us (56%)
  waiting for transfers between devices  174 us (19%)
  blocking collectives  152 us (17%)
  other arithmetic  27.6 us (3%)
  starting transfers between devices  16.8 us (2%)
  local copies, waits for them, and re-layouts  11.9 us (1%)
    pallas_call x16, Pallas kernels, pair(): res = call(*ins)  482 us
    ppermute x26, waiting for transfers between devices, over(): return lax.ppermute(x, 'dp', flip(bit))  174 us
    psum x1, blocking collectives, local_fn(): sums = lax.psum(jnp.sum(st, axis=(1, 2)), 'dp') / total_rows  152 us
    pallas_call x8, Pallas kernels, finish(): pl.pallas_call(functools.partial(finish_kernel, len(parts)), out_shape=ja...  24 us
  transfers between devices with their start and end apart: 26, of which 6 were waited for; matrix products, arithmetic and copies ran while one was open for 3% of the time, Pallas kernels for 25%

profile of v1, /device:TPU:0, one launch (start us, length us, event | category | flops | bytes accessed | tf_op | source)
XLA Modules:
  0.0 892.1 jit_solution(2948509222880351138)
XLA Ops:
  0.6 3.2 fusion.10
  6.1 3.3 collective-permute-start.4
  21.4 3.2 fusion.2
  28.5 46.2 %shard_map.83 = (f32[2048,1024]{1,0:T(8,128)}, f32[2048,1024]{1,0:T(8,128)}, f32[3,8,512]{2,1,0:T(8,128)}) custom-call(f32[2]{0:T(128)} %pad_maximum_fusion.refs_0_, bf16[2048,1024]{1,0:T(8,128)(2,1)} %fusion.1.refs_1_, bf16[2048,1024]{1,0:T(8,128)(2,1)} %fusion.3.refs_2_.refs_3_, f32[3,8,512]{2,1,0:T(8,128)} %broadcast_in_dim.2.refs_3_), custom_call_target="tpu_custom_call" | custom-call | flops 25769803776 | bytes 25165824 | tf_op jit(solution)/shard_map/pallas_call | solution.py:199
  76.8 32.3 %shard_map.84 = (f32[2048,1024]{1,0:T(8,128)}, f32[2048,1024]{1,0:T(8,128)}, f32[512,1024]{1,0:T(8,128)}, f32[3,8,512]{2,1,0:T(8,128)}) custom-call(f32[2]{0:T(128)} %pad_maximum_fusion.refs_0_, bf16[2048,1024]{1,0:T(8,128)(2,1)} %fusion.1.refs_1_, bf16[2048,1024]{1,0:T(8,128)(2,1)} %collective-permute-done.refs_2_.refs_1_, ...), custom_call_target="tpu_custom_call", output_to_operand_aliasing={{0}: (4, {})} | custom-call | flops 12884901888 | bytes 28311552 | tf_op jit(solution)/shard_map/pallas_call | solution.py:199
  109.7 28.7 %shard_map.85 = (f32[512,1024]{1,0:T(8,128)}, f32[512,1024]{1,0:T(8,128)}, f32[2048,1024]{1,0:T(8,128)}, f32[3,8,512]{2,1,0:T(8,128)}) custom-call(f32[2]{0:T(128)} %pad_maximum_fusion.refs_0_, bf16[512,1024]{1,0:T(8,128)(2,1)} %collective-permute-done.5.refs_1_, bf16[512,1024]{1,0:T(8,128)(2,1)} %collective-permute-done.6.refs_2_, ...), custom_call_target="tpu_custom_call", output_to_operand_aliasing={{2}: (4, {})} | custom-call | flops 12884901888 | bytes 18874368 | tf_op jit(solution)/shard_map/pallas_call | solution.py:199
  139.0 6.3 collective-permute-done.9.refs_3_.refs_1_
  145.3 34.6 %shard_map.86 = (f32[2048,1024]{1,0:T(8,128)}, f32[2048,1024]{1,0:T(8,128)}, f32[512,1024]{1,0:T(8,128)}, f32[3,8,512]{2,1,0:T(8,128)}) custom-call(f32[2]{0:T(128)} %pad_maximum_fusion.refs_0_, bf16[2048,1024]{1,0:T(8,128)(2,1)} %fusion.1.refs_1_, ...), custom_call_target="tpu_custom_call", output_to_operand_aliasing={{0}: (4, {}), {1}: (5, {})} | custom-call | flops 12884901888 | bytes 28311552 | tf_op jit(solution)/shard_map/pallas_call | solution.py:199
  180.0 28.7 %shard_map.87 = (f32[512,1024]{1,0:T(8,128)}, f32[512,1024]{1,0:T(8,128)}, f32[2048,1024]{1,0:T(8,128)}, f32[3,8,512]{2,1,0:T(8,128)}) custom-call(f32[2]{0:T(128)} %pad_maximum_fusion.refs_0_, bf16[512,1024]{1,0:T(8,128)(2,1)} %collective-permute-done.11.refs_1_, ...), custom_call_target="tpu_custom_call", output_to_operand_aliasing={{2}: (4, {})} | custom-call | flops 12884901888 | bytes 18874368 | tf_op jit(solution)/shard_map/pallas_call | solution.py:199
  208.7 28.9 %shard_map.88 = (f32[512,1024]{1,0:T(8,128)}, f32[512,1024]{1,0:T(8,128)}, f32[512,1024]{1,0:T(8,128)}, f32[512,1024]{1,0:T(8,128)}, f32[512,1024]{1,0:T(8,128)}...) custom-call(f32[2]{0:T(128)} %pad_maximum_fusion.refs_0_, ...), custom_call_target="tpu_custom_call", output_to_operand_aliasing={{0}: (7, {}), {1}: (8, {}), {2}: (9, {}), {3}: (10, {})} | custom-call | flops 12884901888 | bytes 18874368 | tf_op jit(solution)/shard_map/pallas_call | solution.py:199
  237.7 25.2 %shard_map.89 = (f32[512,1024]{1,0:T(8,128)}, f32[512,1024]{1,0:T(8,128)}, f32[512,1024]{1,0:T(8,128)}, f32[512,1024]{1,0:T(8,128)}, f32[512,1024]{1,0:T(8,128)}...) custom-call(f32[2]{0:T(128)} %pad_maximum_fusion.refs_0_, ...), custom_call_target="tpu_custom_call", output_to_operand_aliasing={{0}: (8, {}), {1}: (9, {}), {6}: (10, {})} | custom-call | flops 9663676416 | bytes 22020096 | tf_op jit(solution)/shard_map/pallas_call | solution.py:199
  262.9 23.8 %shard_map.90 = (f32[512,1024]{1,0:T(8,128)}, f32[512,1024]{1,0:T(8,128)}, f32[512,1024]{1,0:T(8,128)}, f32[512,1024]{1,0:T(8,128)}, f32[512,1024]{1,0:T(8,128)}, /*index=5*/f32[3,8,512]{2,1,0:T(8,128)}) custom-call(f32[2]{0:T(128)} %pad_maximum_fusion.refs_0_, ...), custom_call_target="tpu_custom_call", output_to_operand_aliasing={{0}: (6, {}), {1}: (7, {}), {2}: (8, {}), {3}: (9, {}), {4}... | custom-call | flops 9663676416 | bytes 15728640 | tf_op jit(solution)/shard_map/pallas_call | solution.py:199
  286.6 19.6 %shard_map.91 = (f32[512,1024]{1,0:T(8,128)}, f32[512,1024]{1,0:T(8,128)}, f32[512,1024]{1,0:T(8,128)}, f32[512,1024]{1,0:T(8,128)}, f32[512,1024]{1,0:T(8,128)}, /*index=5*/f32[3,8,512]{2,1,0:T(8,128)}) custom-call(f32[2]{0:T(128)} %pad_maximum_fusion.refs_0_, ...), custom_call_target="tpu_custom_call", output_to_operand_aliasing={{0}: (6, {}), {1}: (7, {}), {2}: (8, {}), {3}: (9, {}), {4}... | custom-call | flops 6442450944 | bytes 15728640 | tf_op jit(solution)/shard_map/pallas_call | solution.py:199
  306.2 30.3 %shard_map.92 = (f32[512,1024]{1,0:T(8,128)}, f32[512,1024]{1,0:T(8,128)}, f32[2048,1024]{1,0:T(8,128)}, f32[3,8,512]{2,1,0:T(8,128)}) custom-call(f32[2]{0:T(128)} %pad_maximum_fusion.refs_0_, bf16[512,1024]{1,0:T(8,128)(2,1)} %collective-permute-done.9.refs_3_.refs_1_, ...), custom_call_target="tpu_custom_call", output_to_operand_aliasing={{0}: (4, {}), {1}: (5, {}), {2}: (6, {})} | custom-call | flops 12884901888 | bytes 18874368 | tf_op jit(solution)/shard_map/pallas_call | solution.py:199
  336.5 17.4 %shard_map.93 = (f32[512,1024]{1,0:T(8,128)}, f32[512,1024]{1,0:T(8,128)}, f32[512,1024]{1,0:T(8,128)}, f32[512,1024]{1,0:T(8,128)}, f32[3,8,512]{2,1,0:T(8,128)}) custom-call(f32[2]{0:T(128)} %pad_maximum_fusion.refs_0_, ...), custom_call_target="tpu_custom_call", output_to_operand_aliasing={{0}: (5, {}), {1}: (6, {}), {2}: (7, {}), {3}: (8, {})} | custom-call | flops 6442450944 | bytes 12582912 | tf_op jit(solution)/shard_map/pallas_call | solution.py:199
  354.0 30.3 %shard_map.94 = (f32[512,1024]{1,0:T(8,128)}, f32[512,1024]{1,0:T(8,128)}, f32[2048,1024]{1,0:T(8,128)}, f32[3,8,512]{2,1,0:T(8,128)}) custom-call(f32[2]{0:T(128)} %pad_maximum_fusion.refs_0_, bf16[512,1024]{1,0:T(8,128)(2,1)} %collective-permute-done.7.refs_5_.refs_3_.refs_1_, ...), custom_call_target="tpu_custom_call", output_to_operand_aliasing={{0}: (4, {}), {1}: (5, {}), {2}: (6, {})} | custom-call | flops 12884901888 | bytes 18874368 | tf_op jit(solution)/shard_map/pallas_call | solution.py:199
  384.3 17.5 %shard_map.95 = (f32[512,1024]{1,0:T(8,128)}, f32[512,1024]{1,0:T(8,128)}, f32[512,1024]{1,0:T(8,128)}, f32[512,1024]{1,0:T(8,128)}, f32[3,8,512]{2,1,0:T(8,128)}) custom-call(f32[2]{0:T(128)} %pad_maximum_fusion.refs_0_, ...), custom_call_target="tpu_custom_call", output_to_operand_aliasing={{0}: (5, {}), {1}: (6, {}), {2}: (7, {}), {3}: (8, {})} | custom-call | flops 6442450944 | bytes 12582912 | tf_op jit(solution)/shard_map/pallas_call | solution.py:199
  401.8 35.7 %shard_map.96 = (f32[2048,1024]{1,0:T(8,128)}, f32[2048,1024]{1,0:T(8,128)}, f32[512,1024]{1,0:T(8,128)}, f32[3,8,512]{2,1,0:T(8,128)}) custom-call(f32[2]{0:T(128)} %pad_maximum_fusion.refs_0_, bf16[2048,1024]{1,0:T(8,128)(2,1)} %fusion.1.refs_1_, ...), custom_call_target="tpu_custom_call", output_to_operand_aliasing={{0}: (4, {}), {1}: (5, {}), {2}: (6, {})} | custom-call | flops 12884901888 | bytes 28311552 | tf_op jit(solution)/shard_map/pallas_call | solution.py:199
  437.5 35.7 %shard_map.97 = (f32[2048,1024]{1,0:T(8,128)}, f32[2048,1024]{1,0:T(8,128)}, f32[512,1024]{1,0:T(8,128)}, f32[3,8,512]{2,1,0:T(8,128)}) custom-call(f32[2]{0:T(128)} %pad_maximum_fusion.refs_0_, bf16[2048,1024]{1,0:T(8,128)(2,1)} %fusion.1.refs_1_, ...), custom_call_target="tpu_custom_call", output_to_operand_aliasing={{0}: (4, {}), {1}: (5, {}), {2}: (6, {})} | custom-call | flops 12884901888 | bytes 28311552 | tf_op jit(solution)/shard_map/pallas_call | solution.py:199
  473.1 46.8 %shard_map.98 = (f32[2048,1024]{1,0:T(8,128)}, f32[2048,1024]{1,0:T(8,128)}, f32[3,8,512]{2,1,0:T(8,128)}) custom-call(f32[2]{0:T(128)} %pad_maximum_fusion.refs_0_, bf16[2048,1024]{1,0:T(8,128)(2,1)} %collective-permute-done.refs_2_.refs_1_, bf16[2048,1024]{1,0:T(8,128)(2,1)} %fusion.3.refs_2_.refs_3_, ...), custom_call_target="tpu_custom_call", output_to_operand_aliasing={{0}: (3, {}), {1}: (4, {})} | custom-call | flops 25769803776 | bytes 25165824 | tf_op jit(solution)/shard_map/pallas_call | solution.py:199
  522.5 13.9 %collective-permute-done.20 = f32[512,1024]{1,0:T(8,128)S(1)} collective-permute-done((f32[512,1024]{1,0:T(8,128)}, f32[512,1024]{1,0:T(8,128)S(1)}, u32[]{:S(2)}, u32[]{:S(2)}) %collective-permute-start.20) | collective-permute-done | bytes 2097184 | tf_op jit(solution)/shard_map/ppermute | solution.py:269
  537.0 32.2 %collective-permute-done.25.refs_3_ = f32[512,1024]{1,0:T(8,128)S(1)} collective-permute-done((f32[512,1024]{1,0:T(8,128)}, f32[512,1024]{1,0:T(8,128)S(1)}, u32[]{:S(2)}, u32[]{:S(2)}) %collective-permute-start.25) | collective-permute-done | bytes 2097184 | tf_op jit(solution)/shard_map/ppermute | solution.py:269
  569.2 44.9 %collective-permute-done.24.refs_3_ = f32[512,1024]{1,0:T(8,128)S(1)} collective-permute-done((f32[512,1024]{1,0:T(8,128)}, f32[512,1024]{1,0:T(8,128)S(1)}, u32[]{:S(2)}, u32[]{:S(2)}) %collective-permute-start.24) | collective-permute-done | bytes 2097184 | tf_op jit(solution)/shard_map/ppermute | solution.py:269
  616.1 3.4 add.17
  619.5 39.6 %collective-permute-done.22.refs_3_ = f32[512,1024]{1,0:T(8,128)S(1)} collective-permute-done((f32[512,1024]{1,0:T(8,128)}, f32[512,1024]{1,0:T(8,128)S(1)}, u32[]{:S(2)}, u32[]{:S(2)}) %collective-permute-start.22) | collective-permute-done | bytes 2097184 | tf_op jit(solution)/shard_map/ppermute | solution.py:269
  667.0 36.6 %collective-permute-done.23.refs_3_ = f32[512,1024]{1,0:T(8,128)S(1)} collective-permute-done((f32[512,1024]{1,0:T(8,128)}, f32[512,1024]{1,0:T(8,128)S(1)}, u32[]{:S(2)}, u32[]{:S(2)}) %collective-permute-start.23) | collective-permute-done | bytes 2097184 | tf_op jit(solution)/shard_map/ppermute | solution.py:269
  705.5 152.2 %psum.7 = f32[3]{0:T(128)S(1)} all-reduce(f32[3]{0:T(128)S(1)} %reduce_sum.109), channel_id=1, replica_groups=mesh['dp'=8] {'dp'}, use_global_device_ids=true, to_apply=%region_11.0 | all-reduce | flops 3 | bytes 24 | tf_op jit(solution)/shard_map/psum | solution.py:313
  861.2 3.4 copy-done.5
  876.3 3.6 shard_map.99.refs_5_
  879.9 3.6 shard_map.100.refs_5_
  883.5 3.6 shard_map.101.refs_5_
  887.2 3.6 shard_map.102
  (111 shorter events, 49.2 us)
Async XLA Ops:
  4.1 7.3 copy-start.3
  6.1 68.7 %collective-permute-start.4 = (bf16[512,1024]{1,0:T(8,128)(2,1)}, bf16[512,1024]{1,0:T(8,128)(2,1)}, u32[]{:S(2)}, u32[]{:S(2)}) collective-permute-start(bf16[512,1024]{1,0:T(8,128)(2,1)} %get-tuple-element.167), channel_id=1, source_target_pairs={{0,4},{1,5},{2,6},{3,7},{4,0},{5,1},{6,2},{7,3}} | collective-permute-start | bytes 3145736 | tf_op jit(solution)/shard_map/ppermute | solution.py:269
  9.4 199.3 %collective-permute-start.1 = (bf16[512,1024]{1,0:T(8,128)(2,1)}, bf16[512,1024]{1,0:T(8,128)(2,1)}, u32[]{:S(2)}, u32[]{:S(2)}) collective-permute-start(bf16[512,1024]{1,0:T(8,128)(2,1)} %get-tuple-element.168), channel_id=1, source_target_pairs={{0,4},{1,5},{2,6},{3,7},{4,0},{5,1},{6,2},{7,3}} | collective-permute-start | bytes 3145736 | tf_op jit(solution)/shard_map/ppermute | solution.py:269
  9.4 129.0 %collective-permute-start.3 = (bf16[512,1024]{1,0:T(8,128)(2,1)}, bf16[512,1024]{1,0:T(8,128)(2,1)}, u32[]{:S(2)}, u32[]{:S(2)}) collective-permute-start(bf16[512,1024]{1,0:T(8,128)(2,1)} %get-tuple-element.170), channel_id=1, source_target_pairs={{0,4},{1,5},{2,6},{3,7},{4,0},{5,1},{6,2},{7,3}} | collective-permute-start | bytes 3145736 | tf_op jit(solution)/shard_map/ppermute | solution.py:269
  15.1 61.7 %collective-permute-start = (bf16[2048,1024]{1,0:T(8,128)(2,1)}, bf16[2048,1024]{1,0:T(8,128)(2,1)}, u32[]{:S(2)}, u32[]{:S(2)}) collective-permute-start(bf16[2048,1024]{1,0:T(8,128)(2,1)} %fusion.1.refs_1_), channel_id=1, source_target_pairs={{0,1},{1,0},{2,3},{3,2},{4,5},{5,4},{6,7},{7,6}} | collective-permute-start | bytes 12582920 | tf_op jit(solution)/shard_map/ppermute | solution.py:269
  18.5 56.8 %collective-permute-start.5 = (bf16[512,1024]{1,0:T(8,128)(2,1)}, bf16[512,1024]{1,0:T(8,128)(2,1)}, u32[]{:S(2)}, u32[]{:S(2)}) collective-permute-start(bf16[512,1024]{1,0:T(8,128)(2,1)} %get-tuple-element.164), channel_id=1, source_target_pairs={{0,2},{1,3},{2,0},{3,1},{4,6},{5,7},{6,4},{7,5}} | collective-permute-start | bytes 3145736 | tf_op jit(solution)/shard_map/ppermute | solution.py:269
  74.8 63.7 %collective-permute-start.11 = (bf16[512,1024]{1,0:T(8,128)(2,1)}, bf16[512,1024]{1,0:T(8,128)(2,1)}, u32[]{:S(2)}, u32[]{:S(2)}) collective-permute-start(bf16[512,1024]{1,0:T(8,128)(2,1)} %get-tuple-element.163), channel_id=1, source_target_pairs={{0,2},{1,3},{2,0},{3,1},{4,6},{5,7},{6,4},{7,5}} | collective-permute-start | bytes 3145736 | tf_op jit(solution)/shard_map/ppermute | solution.py:269
  75.3 63.4 %collective-permute-start.7 = (bf16[512,1024]{1,0:T(8,128)(2,1)}, bf16[512,1024]{1,0:T(8,128)(2,1)}, u32[]{:S(2)}, u32[]{:S(2)}) collective-permute-start(bf16[512,1024]{1,0:T(8,128)(2,1)} %get-tuple-element.165), channel_id=1, source_target_pairs={{0,2},{1,3},{2,0},{3,1},{4,6},{5,7},{6,4},{7,5}} | collective-permute-start | bytes 3145736 | tf_op jit(solution)/shard_map/ppermute | solution.py:269
  76.8 32.3 %collective-permute-start.6 = (bf16[512,1024]{1,0:T(8,128)(2,1)}, bf16[512,1024]{1,0:T(8,128)(2,1)}, u32[]{:S(2)}, u32[]{:S(2)}) collective-permute-start(bf16[512,1024]{1,0:T(8,128)(2,1)} %collective-permute-done.5.refs_1_), channel_id=1, source_target_pairs={{0,1},{1,0},{2,3},{3,2},{4,5},{5,4},{6,7},{7,6}} | collective-permute-start | bytes 3145736 | tf_op jit(solution)/shard_map/ppermute | solution.py:269
  109.1 36.2 %collective-permute-start.9 = (bf16[512,1024]{1,0:T(8,128)(2,1)}, bf16[512,1024]{1,0:T(8,128)(2,1)}, u32[]{:S(2)}, u32[]{:S(2)}) collective-permute-start(bf16[512,1024]{1,0:T(8,128)(2,1)} %get-tuple-element.166), channel_id=1, source_target_pairs={{0,2},{1,3},{2,0},{3,1},{4,6},{5,7},{6,4},{7,5}} | collective-permute-start | bytes 3145736 | tf_op jit(solution)/shard_map/ppermute | solution.py:269
  138.4 70.3 %collective-permute-start.2 = (bf16[512,1024]{1,0:T(8,128)(2,1)S(1)}, bf16[512,1024]{1,0:T(8,128)(2,1)}, u32[]{:S(2)}, u32[]{:S(2)}) collective-permute-start(bf16[512,1024]{1,0:T(8,128)(2,1)S(1)} %get-tuple-element.169), channel_id=1, source_target_pairs={{0,4},{1,5},{2,6},{3,7},{4,0},{5,1},{6,2},{7,3}} | collective-permute-start | bytes 3145736 | tf_op jit(solution)/shard_map/ppermute | solution.py:269
  138.5 41.5 %collective-permute-start.12 = (bf16[512,1024]{1,0:T(8,128)(2,1)}, bf16[512,1024]{1,0:T(8,128)(2,1)}, u32[]{:S(2)}, u32[]{:S(2)}) collective-permute-start(bf16[512,1024]{1,0:T(8,128)(2,1)} %collective-permute-done.11.refs_1_), channel_id=1, source_target_pairs={{0,1},{1,0},{2,3},{3,2},{4,5},{5,4},{6,7},{7,6}} | collective-permute-start | bytes 3145736 | tf_op jit(solution)/shard_map/ppermute | solution.py:269
  138.7 99.0 %collective-permute-start.8 = (bf16[512,1024]{1,0:T(8,128)(2,1)}, bf16[512,1024]{1,0:T(8,128)(2,1)}, u32[]{:S(2)}, u32[]{:S(2)}) collective-permute-start(bf16[512,1024]{1,0:T(8,128)(2,1)} %collective-permute-done.7.refs_5_.refs_3_.refs_1_), channel_id=1, source_target_pairs={{0,1},{1,0},{2,3},{3,2},{4,5},{5,4},{6,7},{7,6}} | collective-permute-start | bytes 3145736 | tf_op jit(solution)/shard_map/ppermute | solution.py:269
  145.3 92.4 %collective-permute-start.10 = (bf16[512,1024]{1,0:T(8,128)(2,1)}, bf16[512,1024]{1,0:T(8,128)(2,1)}, u32[]{:S(2)}, u32[]{:S(2)}) collective-permute-start(bf16[512,1024]{1,0:T(8,128)(2,1)} %collective-permute-done.9.refs_3_.refs_1_), channel_id=1, source_target_pairs={{0,1},{1,0},{2,3},{3,2},{4,5},{5,4},{6,7},{7,6}} | collective-permute-start | bytes 3145736 | tf_op jit(solution)/shard_map/ppermute | solution.py:269
  520.0 354.1 %collective-permute-start.13 = (f32[2048,1024]{1,0:T(8,128)}, f32[2048,1024]{1,0:T(8,128)}, u32[]{:S(2)}, u32[]{:S(2)}) collective-permute-start(f32[2048,1024]{1,0:T(8,128)} %get-tuple-element.141), channel_id=1, source_target_pairs={{0,1},{1,0},{2,3},{3,2},{4,5},{5,4},{6,7},{7,6}} | collective-permute-start | bytes 25165832 | tf_op jit(solution)/shard_map/ppermute | solution.py:269
  520.5 16.0 %collective-permute-start.20 = (f32[512,1024]{1,0:T(8,128)}, f32[512,1024]{1,0:T(8,128)S(1)}, u32[]{:S(2)}, u32[]{:S(2)}) collective-permute-start(f32[512,1024]{1,0:T(8,128)} %get-tuple-element.149), channel_id=1, source_target_pairs={{0,1},{1,0},{2,3},{3,2},{4,5},{5,4},{6,7},{7,6}} | collective-permute-start | bytes 6291464 | tf_op jit(solution)/shard_map/ppermute | solution.py:269
  520.5 48.7 %collective-permute-start.25 = (f32[512,1024]{1,0:T(8,128)}, f32[512,1024]{1,0:T(8,128)S(1)}, u32[]{:S(2)}, u32[]{:S(2)}) collective-permute-start(f32[512,1024]{1,0:T(8,128)} %get-tuple-element.154), channel_id=1, source_target_pairs={{0,4},{1,5},{2,6},{3,7},{4,0},{5,1},{6,2},{7,3}} | collective-permute-start | bytes 6291464 | tf_op jit(solution)/shard_map/ppermute | solution.py:269
  521.0 93.1 %collective-permute-start.24 = (f32[512,1024]{1,0:T(8,128)}, f32[512,1024]{1,0:T(8,128)S(1)}, u32[]{:S(2)}, u32[]{:S(2)}) collective-permute-start(f32[512,1024]{1,0:T(8,128)} %get-tuple-element.153), channel_id=1, source_target_pairs={{0,4},{1,5},{2,6},{3,7},{4,0},{5,1},{6,2},{7,3}} | collective-permute-start | bytes 6291464 | tf_op jit(solution)/shard_map/ppermute | solution.py:269
  522.5 93.0 %collective-permute-start.18 = (f32[512,1024]{1,0:T(8,128)}, f32[512,1024]{1,0:T(8,128)S(1)}, u32[]{:S(2)}, u32[]{:S(2)}) collective-permute-start(f32[512,1024]{1,0:T(8,128)} %get-tuple-element.147), channel_id=1, source_target_pairs={{0,1},{1,0},{2,3},{3,2},{4,5},{5,4},{6,7},{7,6}} | collective-permute-start | bytes 6291464 | tf_op jit(solution)/shard_map/ppermute | solution.py:269
  536.5 122.6 %collective-permute-start.22 = (f32[512,1024]{1,0:T(8,128)}, f32[512,1024]{1,0:T(8,128)S(1)}, u32[]{:S(2)}, u32[]{:S(2)}) collective-permute-start(f32[512,1024]{1,0:T(8,128)} %get-tuple-element.151), channel_id=1, source_target_pairs={{0,4},{1,5},{2,6},{3,7},{4,0},{5,1},{6,2},{7,3}} | collective-permute-start | bytes 6291464 | tf_op jit(solution)/shard_map/ppermute | solution.py:269
  569.2 92.2 %collective-permute-start.16 = (f32[512,1024]{1,0:T(8,128)}, f32[512,1024]{1,0:T(8,128)S(1)}, u32[]{:S(2)}, u32[]{:S(2)}) collective-permute-start(f32[512,1024]{1,0:T(8,128)} %get-tuple-element.145), channel_id=1, source_target_pairs={{0,1},{1,0},{2,3},{3,2},{4,5},{5,4},{6,7},{7,6}} | collective-permute-start | bytes 6291464 | tf_op jit(solution)/shard_map/ppermute | solution.py:269
  615.5 49.2 %collective-permute-start.14 = (f32[512,1024]{1,0:T(8,128)}, f32[512,1024]{1,0:T(8,128)S(1)}, u32[]{:S(2)}, u32[]{:S(2)}) collective-permute-start(f32[512,1024]{1,0:T(8,128)} %get-tuple-element.143), channel_id=1, source_target_pairs={{0,1},{1,0},{2,3},{3,2},{4,5},{5,4},{6,7},{7,6}} | collective-permute-start | bytes 6291464 | tf_op jit(solution)/shard_map/ppermute | solution.py:269
  615.5 88.0 %collective-permute-start.23 = (f32[512,1024]{1,0:T(8,128)}, f32[512,1024]{1,0:T(8,128)S(1)}, u32[]{:S(2)}, u32[]{:S(2)}) collective-permute-start(f32[512,1024]{1,0:T(8,128)} %get-tuple-element.152), channel_id=1, source_target_pairs={{0,4},{1,5},{2,6},{3,7},{4,0},{5,1},{6,2},{7,3}} | collective-permute-start | bytes 6291464 | tf_op jit(solution)/shard_map/ppermute | solution.py:269
  616.1 43.6 %copy-start.13 = (f32[512,1024]{1,0:T(8,128)S(1)}, f32[512,1024]{1,0:T(8,128)}, u32[]{:S(2)}) copy-start(f32[512,1024]{1,0:T(8,128)} %get-tuple-element.146) | copy-start | bytes 6291460
  659.1 215.0 %collective-permute-start.21 = (f32[512,1024]{1,0:T(8,128)}, f32[512,1024]{1,0:T(8,128)}, u32[]{:S(2)}, u32[]{:S(2)}) collective-permute-start(f32[512,1024]{1,0:T(8,128)} %add.17), channel_id=1, source_target_pairs={{0,2},{1,3},{2,0},{3,1},{4,6},{5,7},{6,4},{7,5}} | collective-permute-start | bytes 6291464 | tf_op jit(solution)/shard_map/ppermute | solution.py:269
  661.4 218.5 %collective-permute-start.19 = (f32[512,1024]{1,0:T(8,128)}, f32[512,1024]{1,0:T(8,128)}, u32[]{:S(2)}, u32[]{:S(2)}) collective-permute-start(f32[512,1024]{1,0:T(8,128)} %add.16), channel_id=1, source_target_pairs={{0,2},{1,3},{2,0},{3,1},{4,6},{5,7},{6,4},{7,5}} | collective-permute-start | bytes 6291464 | tf_op jit(solution)/shard_map/ppermute | solution.py:269
  664.7 218.9 %collective-permute-start.17 = (f32[512,1024]{1,0:T(8,128)}, f32[512,1024]{1,0:T(8,128)}, u32[]{:S(2)}, u32[]{:S(2)}) collective-permute-start(f32[512,1024]{1,0:T(8,128)} %add.15), channel_id=1, source_target_pairs={{0,2},{1,3},{2,0},{3,1},{4,6},{5,7},{6,4},{7,5}} | collective-permute-start | bytes 6291464 | tf_op jit(solution)/shard_map/ppermute | solution.py:269
  665.2 40.2 %copy-start.16 = (f32[3,8,512]{2,1,0:T(8,128)S(1)}, f32[3,8,512]{2,1,0:T(8,128)}, u32[]{:S(2)}) copy-start(f32[3,8,512]{2,1,0:T(8,128)} %get-tuple-element.139) | copy-start | bytes 147460
  665.2 193.8 %copy-start.12 = (f32[2]{0:T(128)S(1)}, f32[2]{0:T(128)}, u32[]{:S(2)}) copy-start(f32[2]{0:T(128)} %pad_maximum_fusion.refs_0_) | copy-start | bytes 28
  704.9 182.3 %collective-permute-start.15 = (f32[512,1024]{1,0:T(8,128)}, f32[512,1024]{1,0:T(8,128)}, u32[]{:S(2)}, u32[]{:S(2)}) collective-permute-start(f32[512,1024]{1,0:T(8,128)} %add.14), channel_id=1, source_target_pairs={{0,2},{1,3},{2,0},{3,1},{4,6},{5,7},{6,4},{7,5}} | collective-permute-start | bytes 6291464 | tf_op jit(solution)/shard_map/ppermute | solution.py:269
  869.3 4.8 slice-start
  871.7 4.6 slice-start.1
  (13 other events, 34.0 us)
